TPU v7x, 8 devices: a whole 2x2x1 slice. The times are simulated.
8 devices in a mesh: dp: 1 (over z), tp: 2 (over y), sp: 4 (over x, core).
Axes of the slice: x: 2, y: 2, z: 1, core: 2. Of those that a mesh axis runs over, the one named last changes fastest.
Arguments:
- x_in: bfloat16 [4096, 768], P(('dp', 'sp'))
- w_z: bfloat16 [768, 1536], P(None, 'tp')
- w_x: bfloat16 [768, 1536], P(None, 'tp')
- w_bc: bfloat16 [768, 256], replicated
- w_dt: bfloat16 [768, 24], P(None, 'tp')
- a_neg: float32 [24], P('tp')
- dt_bias: float32 [24], P('tp')
- d_skip: float32 [24], P('tp')
- w_out: bfloat16 [1536, 768], P('tp')
Outputs:
- output: bfloat16 [4096, 768], P(('dp', 'sp', 'tp'))
All inputs are finite; a program needn't handle non-finite values.
Results may differ from a plain program's by a relative error of at most 0.0111934.
Values are sent between devices in bfloat16 or wider.
A program may use at most 1 GiB of HBM per device.

v0:
```python
import jax
import jax.numpy as jnp
from jax import lax
from jax.experimental import pallas as pl
from jax.experimental.pallas import tpu as pltpu
from jax.sharding import PartitionSpec as P

MESH = pl.DeviceIdType.MESH
F32 = jnp.float32
BF16 = jnp.bfloat16
LOG2E = 1.4426950408889634

CHUNK = 128
LANES = 128
GROUP_COLS = 256


def dot(a, b):
    return jnp.dot(a, b, preferred_element_type=F32)


def split3(v):
    hi = v.astype(BF16)
    rest = v - hi.astype(F32)
    mid = rest.astype(BF16)
    return hi, mid, (rest - mid.astype(F32)).astype(BF16)


def softplus(v):
    return jnp.maximum(v, 0.0) + jnp.log1p(jnp.exp(-jnp.abs(v)))


def kernel(dims, x_hbm, wz_hbm, wx_hbm, wbc_hbm, wdt_hbm, wo_hbm, a_s, bias_s, dskip_s, out_ref,
           x_v, wz_v, wx_v, wbc_v, wdt_v, wo_own, wo_peer, c_v, bt_v, rpad_v, dt_v, ct_v, et_v, cola_v, colb_v, colc_v,
           elo_v, ehi_v, tab_v, gram_v, u_v, z_v, y_v, pf_v, pb_v, hf_v, hb_v, s1_send, s1_recv, dec_send, dec_recv,
           s2_send, s2_recv, g_v, g_recv, acc_v,
           in_sem, s1_ss, s1_rs, dec_ss, dec_rs, s2_ss, s2_rs, wy_ss, wy_rs, wf_ss, wf_rs, g_ss, g_rs):
    tokens, n_head, n_sp = dims
    d_model = x_v.shape[1]
    inner = wx_v.shape[1]
    n_chunk = tokens // CHUNK
    n_half = n_chunk // 2
    half = tokens // 2
    n_grp = inner // GROUP_COLS
    head_dim = inner // n_head
    grp_heads = GROUP_COLS // head_dim
    wrows = inner // n_sp

    tp = lax.axis_index('tp')
    sp = lax.axis_index('sp')
    core = lax.rem(sp, 2)
    partner = sp + 1 - 2 * core
    other_tp = 1 - tp
    my_base = tp * n_half
    peer_base = other_tp * n_half

    def load(src, dst, i):
        return pltpu.make_async_copy(src, dst, in_sem.at[i])

    ld_bc = load(wbc_hbm, wbc_v, 0)
    ld_dt = load(wdt_hbm, wdt_v, 1)
    ld_x = [load(x_hbm.at[pl.ds(i * half, half)], x_v.at[pl.ds(i * half, half)], 2 + i) for i in range(2)]
    ld_wx = load(wx_hbm, wx_v, 4)
    ld_wz = load(wz_hbm, wz_v, 5)
    ld_wo = load(wo_hbm, wo_own, 6)
    for ld in (ld_bc, ld_dt, ld_x[0], ld_x[1], ld_wx, ld_wz):
        ld.start()

    barrier = pltpu.get_barrier_semaphore()
    for step in range(1, n_sp):
        pl.semaphore_signal(barrier, inc=1, device_id={'sp': lax.rem(sp + step, n_sp)}, device_id_type=MESH)
    pl.semaphore_signal(barrier, inc=1, device_id={'tp': other_tp}, device_id_type=MESH)

    row_h = lax.broadcasted_iota(jnp.int32, (16, LANES), 0)
    bias_t = jnp.zeros((16, LANES), F32)
    a_t = jnp.zeros((16, LANES), F32)
    for h in range(n_head):
        bias_t = jnp.where(row_h == h, bias_s[h], bias_t)
        a_t = jnp.where(row_h == h, a_s[h] * LOG2E, a_t)
    sq_r = lax.broadcasted_iota(jnp.int32, (CHUNK, LANES), 0)
    sq_c = lax.broadcasted_iota(jnp.int32, (CHUNK, LANES), 1)
    tri = jnp.concatenate([jnp.where(sq_r <= sq_c, 1.0, 0.0), jnp.where(sq_r < sq_c, 1.0, 0.0)], axis=1).astype(BF16)
    diag2 = jnp.where(sq_r == sq_c, 2.0, 1.0)
    ex_r = lax.broadcasted_iota(jnp.int32, (LANES, inner), 0)
    ex_h = lax.broadcasted_iota(jnp.int32, (LANES, inner), 1) // head_dim
    ex_q = jnp.where(lax.rem(ex_r, 16) == ex_h, 1.0, 0.0)
    elo_v[...] = jnp.where(ex_r < 48, ex_q, 0.0).astype(BF16)
    ehi_v[...] = jnp.where((ex_r >= 64) & (ex_r < 112), ex_q, 0.0).astype(BF16)
    e_one = jnp.where(ex_r[:32] == ex_h[:32], 1.0, 0.0).astype(BF16)
    rpad_v[...] = jnp.zeros_like(rpad_v)

    pl.semaphore_wait(barrier, n_sp)

    my_rows = pl.ds(sp * wrows, wrows)
    wy = pltpu.make_async_remote_copy(src_ref=wo_hbm.at[my_rows], dst_ref=wo_peer.at[my_rows], send_sem=wy_ss, recv_sem=wy_rs,
                                      device_id={'tp': other_tp}, device_id_type=MESH)
    wy.start()

    ld_bc.wait()
    ld_dt.wait()
    for i in range(2):
        ld_x[i].wait()
        rows = slice(i * half, (i + 1) * half)
        x_half = x_v[rows, :]
        bc_val = dot(x_half, wbc_v[...]).astype(BF16)
        c_v[rows, :] = bc_val[:, LANES:]
        rpad_v[rows, 0:n_head] = lax.dot_general(x_half, wdt_v[...], (((1,), (1,)), ((), ())), preferred_element_type=F32)
        for k in range(n_half):
            c = i * n_half + k
            bt_v[c] = bc_val[k * CHUNK:(k + 1) * CHUNK, :LANES].astype(F32).T.astype(BF16)
            dt_v[c] = softplus(rpad_v[c * CHUNK:(c + 1) * CHUNK, :].T[:16] + bias_t)
    ld_wo.start()

    dt_all = dt_v[...].reshape(n_chunk * 16, LANES)
    la_all = (dt_v[...] * a_t[None]).reshape(n_chunk * 16, LANES)
    cum = sum(dot(part, tri) for part in split3(la_all))
    c_log = cum[:, :LANES]
    e_log = cum[:, LANES:]
    ct_v[...] = c_log.reshape(n_chunk, 16, LANES)
    et_v[...] = e_log.reshape(n_chunk, 16, LANES)
    tail = c_log[:, LANES - 1:LANES]
    parts_ef = split3(jnp.exp2(c_log))
    parts_eb = split3(jnp.exp2(tail - e_log))
    parts_wf = split3(jnp.exp2(tail - c_log) * dt_all)
    parts_wb = split3(jnp.exp2(e_log) * dt_all)
    blank = jnp.zeros((16, LANES), F32)

    def column_tile(first, second, c):
        rows = slice(c * 16, (c + 1) * 16)
        tile = [p[rows].astype(F32) for p in first] + [blank] + [p[rows].astype(F32) for p in second] + [blank]
        return jnp.concatenate(tile, axis=0).T.astype(BF16)

    run = jnp.zeros((1, 32), F32)
    tails, starts, ends = [], [], []
    for c in range(n_chunk):
        rows = slice(c * 16, (c + 1) * 16)
        colb_v[c] = column_tile(parts_wf, parts_wb, c)
        col = jnp.concatenate([c_log[rows], e_log[rows]], axis=0).T
        colc_v[c] = col
        last = col[CHUNK - 1:CHUNK, :]
        tails.append(last)
        starts.append(run)
        run = run + last
        ends.append(run)
    logs = jnp.concatenate(tails + starts + [run - e for e in ends] + [run] * n_chunk, axis=0)
    tab = sum(dot(part, e_one) for part in split3(jnp.exp2(logs)))
    for i in range(3 * n_chunk + 1):
        tab_v[i] = tab[i:i + 1, :]
    dec_send[...] = tab[3 * n_chunk:, :]
    for c in range(n_chunk):
        cola_v[c] = column_tile(parts_ef, parts_eb, c)

    def to_partner(g):
        return pltpu.make_async_remote_copy(src_ref=s1_send.at[g], dst_ref=s1_recv.at[g], send_sem=s1_ss.at[g], recv_sem=s1_rs.at[g],
                                            device_id={'sp': partner}, device_id_type=MESH)

    def to_chip(g, t):
        return pltpu.make_async_remote_copy(src_ref=s2_send.at[g], dst_ref=s2_recv.at[g], send_sem=s2_ss.at[g, t], recv_sem=s2_rs.at[g],
                                            device_id={'sp': 2 - 2 * (sp // 2) + t}, device_id_type=MESH)

    def to_peer(g, k):
        return pltpu.make_async_remote_copy(src_ref=g_v.at[g, peer_base + k], dst_ref=g_recv.at[g, k], send_sem=g_ss.at[g, k],
                                            recv_sem=g_rs.at[g, k], device_id={'tp': other_tp}, device_id_type=MESH)

    def gather(step):
        return pltpu.make_async_remote_copy(src_ref=wo_peer.at[my_rows], dst_ref=wo_peer.at[my_rows], send_sem=wf_ss.at[step - 1],
                                            recv_sem=wf_rs.at[step - 1], device_id={'sp': lax.rem(sp + step, n_sp)}, device_id_type=MESH)

    dec_copy = pltpu.make_async_remote_copy(src_ref=dec_send, dst_ref=dec_recv, send_sem=dec_ss, recv_sem=dec_rs,
                                            device_id={'sp': partner}, device_id_type=MESH)
    dec_copy.start()

    def states(g):
        cols = slice(g * GROUP_COLS, (g + 1) * GROUP_COLS)
        for i in range(2):
            rows = slice(i * half, (i + 1) * half)
            u_v[g, rows, :] = dot(x_v[rows, :], wx_v[:, cols]).astype(BF16)
        elo = elo_v[:, cols]
        ehi = ehi_v[:, cols]
        st_f, st_b = [], []
        for c in range(n_chunk):
            u_c = u_v[g, c * CHUNK:(c + 1) * CHUNK, :].astype(F32)
            st_f.append(dot(bt_v[c], (u_c * dot(colb_v[c], elo)).astype(BF16)))
            st_b.append(dot(bt_v[c], (u_c * dot(colb_v[c], ehi)).astype(BF16)))
        acc = jnp.zeros((LANES, GROUP_COLS), F32)
        for c in range(n_chunk):
            pf_v[g, c] = acc
            acc = tab_v[c][:, cols] * acc + st_f[c]
        pf_v[g, n_chunk] = acc
        acc = jnp.zeros((LANES, GROUP_COLS), F32)
        for c in reversed(range(n_chunk)):
            pb_v[g, c] = acc
            acc = tab_v[c][:, cols] * acc + st_b[c]
        pb_v[g, n_chunk] = acc
        s1_send[g] = jnp.where(core == 0, pf_v[g, n_chunk], acc).astype(BF16)
        to_partner(g).start()

    sends_far = (sp == 1) | (sp == 2)

    def pass_on(g):
        to_partner(g).wait_recv()

        @pl.when(sends_far)
        def _():
            cols = slice(g * GROUP_COLS, (g + 1) * GROUP_COLS)
            own = jnp.where(core == 1, pf_v[g, n_chunk], pb_v[g, n_chunk])
            s2_send[g] = (own + tab_v[3 * n_chunk][:, cols] * s1_recv[g].astype(F32)).astype(BF16)
            to_chip(g, 0).start()
            to_chip(g, 1).start()

    def incoming(g):
        to_chip(g, 0).wait_recv()
        cols = slice(g * GROUP_COLS, (g + 1) * GROUP_COLS)
        near = s1_recv[g].astype(F32)
        far = s2_recv[g].astype(F32)
        both = near + dec_recv[0:1, cols] * far
        hf_v[g] = jnp.where(sp == 0, 0.0, jnp.where(sp == 1, near, jnp.where(sp == 2, far, both)))
        hb_v[g] = jnp.where(sp == 3, 0.0, jnp.where(sp == 2, near, jnp.where(sp == 1, far, both)))

    lane = lax.broadcasted_iota(jnp.int32, (CHUNK, LANES), 1)
    low_lane = lane < head_dim

    def z_part(g, base):
        cols = slice(g * GROUP_COLS, (g + 1) * GROUP_COLS)
        rows = pl.ds(pl.multiple_of(base * CHUNK, CHUNK), half)
        z_v[g, rows, :] = dot(x_v[rows, :], wz_v[:, cols]).astype(BF16)

    def intra(g, c):
        rows = pl.ds(pl.multiple_of(c * CHUNK, CHUNK), CHUNK)
        gram = gram_v[c]
        for p in range(grp_heads // 2):
            lanes = slice(p * LANES, (p + 1) * LANES)
            u_pair = u_v[g, rows, lanes]
            weights = []
            for h in (g * grp_heads + 2 * p, g * grp_heads + 2 * p + 1):
                arg = jnp.minimum(colc_v[c, :, h:h + 1] - ct_v[c, h:h + 1, :], et_v[c, h:h + 1, :] - colc_v[c, :, 16 + h:17 + h])
                weights.append((gram * jnp.exp2(arg) * dt_v[c, h:h + 1, :]).astype(BF16))
            zero = jnp.zeros_like(u_pair)
            u_diag = jnp.concatenate([jnp.where(low_lane, u_pair, zero), jnp.where(low_lane, zero, u_pair)], axis=0)
            h0 = g * grp_heads + 2 * p
            skip = jnp.where(low_lane[:1], 2.0 * dskip_s[h0], 2.0 * dskip_s[h0 + 1])
            y_v[g, rows, lanes] = dot(jnp.concatenate(weights, axis=1), u_diag) + skip * u_pair.astype(F32)

    def finish(g, c):
        cols = slice(g * GROUP_COLS, (g + 1) * GROUP_COLS)
        rows = pl.ds(pl.multiple_of(c * CHUNK, CHUNK), CHUNK)
        in_f = (pf_v[g, c] + tab_v[n_chunk + c][:, cols] * hf_v[g]).astype(BF16)
        in_b = (pb_v[g, c] + tab_v[2 * n_chunk + c][:, cols] * hb_v[g]).astype(BF16)
        c_mat = c_v[rows, :]
        y = y_v[g, rows, :] + dot(cola_v[c], elo_v[:, cols]) * dot(c_mat, in_f) + dot(cola_v[c], ehi_v[:, cols]) * dot(c_mat, in_b)
        hz = 0.5 * z_v[g, rows, :].astype(F32)
        g_v[g, c] = (y * (hz + hz * jnp.tanh(hz))).astype(BF16)

    ld_wx.wait()
    states(0)
    for c in range(n_chunk):
        gram_v[c] = dot(c_v[c * CHUNK:(c + 1) * CHUNK, :], bt_v[c]) * diag2
    states(1)
    pass_on(0)
    states(2)
    pass_on(1)
    ld_wz.wait()
    z_part(0, peer_base)
    for k in range(n_half):
        intra(0, peer_base + k)
    pass_on(2)
    dec_copy.wait_recv()
    for g in range(n_grp):
        if g > 0:
            z_part(g, peer_base)
            for k in range(n_half):
                intra(g, peer_base + k)
        incoming(g)
        for k in range(n_half):
            finish(g, peer_base + k)
            to_peer(g, k).start()
        if g == 0:
            wy.wait_recv()
            for step in range(1, n_sp):
                gather(step).start()

    for g in range(n_grp):
        z_part(g, my_base)
        for k in range(n_half):
            intra(g, my_base + k)
        for k in range(n_half):
            finish(g, my_base + k)
    ld_wo.wait()
    my_tokens = pl.ds(pl.multiple_of(my_base * CHUNK, CHUNK), half)
    acc_v[...] = x_v[my_tokens, :].astype(F32)
    for g in range(n_grp):
        mine = g_v[g, pl.ds(my_base, n_half)].reshape(half, GROUP_COLS)
        acc_v[...] += dot(mine, wo_own[g * GROUP_COLS:(g + 1) * GROUP_COLS, :])
    for step in range(1, n_sp):
        gather(step).wait_recv()
    for g in range(n_grp):
        w_g = wo_peer[g * GROUP_COLS:(g + 1) * GROUP_COLS, :]
        for k in range(n_half):
            to_peer(g, k).wait_recv()
            rows = slice(k * CHUNK, (k + 1) * CHUNK)
            val = acc_v[rows, :] + dot(g_recv[g, k], w_g)
            if g < n_grp - 1:
                acc_v[rows, :] = val
            else:
                out_ref[rows, :] = val.astype(BF16)

    wy.wait_send()
    dec_copy.wait_send()
    for step in range(1, n_sp):
        gather(step).wait_send()
    for g in range(n_grp):
        to_partner(g).wait_send()

        @pl.when(sends_far)
        def _():
            to_chip(g, 0).wait_send()
            to_chip(g, 1).wait_send()
        for k in range(n_half):
            to_peer(g, k).wait_send()


def solution(mesh):
    n_sp = mesh.shape['sp']

    def device_fn(x_blk, w_z, w_x, w_bc, w_dt, a_neg, dt_bias, d_skip, w_out):
        tokens, d_model = x_blk.shape
        n_head = a_neg.shape[0]
        inner = w_x.shape[1]
        half = tokens // 2
        n_chunk = tokens // CHUNK
        n_half = n_chunk // 2
        n_grp = inner // GROUP_COLS
        vmem = pltpu.VMEM
        dma = pltpu.SemaphoreType.DMA
        state = (n_grp, LANES, GROUP_COLS)
        hbm = pl.BlockSpec(memory_space=pl.ANY)
        smem = pl.BlockSpec(memory_space=pltpu.SMEM)

        def body(*refs):
            kernel((tokens, n_head, n_sp), *refs)

        return pl.pallas_call(
            body,
            out_shape=jax.ShapeDtypeStruct((half, d_model), BF16),
            in_specs=[hbm] * 6 + [smem] * 3,
            out_specs=pl.BlockSpec(memory_space=pltpu.VMEM),
            scratch_shapes=[
                vmem((tokens, d_model), BF16), vmem((d_model, inner), BF16), vmem((d_model, inner), BF16),
                vmem(w_bc.shape, BF16), vmem(w_dt.shape[::-1], BF16), vmem((inner, d_model), BF16), vmem((inner, d_model), BF16),
                vmem((tokens, LANES), BF16), vmem((n_chunk, LANES, CHUNK), BF16), vmem((tokens, LANES), F32),
                vmem((n_chunk, 16, LANES), F32), vmem((n_chunk, 16, LANES), F32), vmem((n_chunk, 16, LANES), F32),
                vmem((n_chunk, CHUNK, LANES), BF16), vmem((n_chunk, CHUNK, LANES), BF16), vmem((n_chunk, CHUNK, 32), F32),
                vmem((LANES, inner), BF16), vmem((LANES, inner), BF16), vmem((3 * n_chunk + 1, 1, inner), F32),
                vmem((n_chunk, CHUNK, CHUNK), F32),
                vmem((n_grp, tokens, GROUP_COLS), BF16), vmem((n_grp, tokens, GROUP_COLS), BF16), vmem((n_grp, tokens, GROUP_COLS), F32),
                vmem((n_grp, n_chunk + 1, LANES, GROUP_COLS), F32), vmem((n_grp, n_chunk + 1, LANES, GROUP_COLS), F32),
                vmem(state, F32), vmem(state, F32), vmem(state, BF16), vmem(state, BF16),
                vmem((8, inner), F32), vmem((8, inner), F32), vmem(state, BF16), vmem(state, BF16),
                vmem((n_grp, n_chunk, CHUNK, GROUP_COLS), BF16), vmem((n_grp, n_half, CHUNK, GROUP_COLS), BF16),
                vmem((half, d_model), F32),
                dma((7,)), dma((n_grp,)), dma((n_grp,)), dma, dma, dma((n_grp, 2)), dma((n_grp,)),
                dma, dma, dma((n_sp - 1,)), dma((n_sp - 1,)), dma((n_grp, n_half)), dma((n_grp, n_half)),
            ],
            compiler_params=pltpu.CompilerParams(collective_id=0, has_side_effects=True),
            cost_estimate=pl.CostEstimate(flops=8 * 10 ** 9, bytes_accessed=8 * 10 ** 6, transcendentals=4 * 10 ** 6),
            name='mamba_layer',
        )(x_blk, w_z, w_x, w_bc, w_dt.T, w_out, a_neg, dt_bias, d_skip)

    in_specs = (P(('dp', 'sp'), None), P(None, 'tp'), P(None, 'tp'), P(None, None), P(None, 'tp'), P('tp'), P('tp'), P('tp'), P('tp', None))
    out_specs = P(('dp', 'sp', 'tp'), None)
    return jax.shard_map(device_fn, mesh=mesh, in_specs=in_specs, out_specs=out_specs, check_vma=False)
```

profile of v0, /device:TPU:0, one launch (start us, length us, event | category | flops | bytes accessed | tf_op | source)
XLA Modules:
  0.0 36.5 jit_solution(13824358597688665182)
XLA Ops:
  0.0 34.4 %mamba_layer.1 = bf16[512,768]{1,0:T(8,128)(2,1)} custom-call(bf16[1024,768]{1,0:T(8,128)(2,1)} %refs_0_.1, bf16[768,768]{1,0:T(8,128)(2,1)} %refs_1_.1, bf16[768,768]{1,0:T(8,128)(2,1)} %refs_2_.1, bf16[768,256]{1,0:T(8,128)(2,1)} %refs_3_.1, bf16[12,768]{1,0:T(8,128)(2,1)} %bitcast.1, bf16[768,768]{1,0:T(8,128)(2,1)} %refs_5_.1, f32[12]{0:T(128)} %refs_6_.1, ...), custom_call_target="tpu_custom_call" | custom-call | flops 8000000000 | bytes 8000000 | tf_op jit(solution)/shard_map/mamba_layer/pallas_call | solution.py:342
  34.4 2.1 %copy.11 = bf16[512,768]{1,0:T(8,128)(2,1)} copy(bf16[512,768]{1,0:T(8,128)(2,1)} %mamba_layer.1) | data formatting | bytes 1572864
where the time goes:
time: 36.6 us; the launch traced here: 36.5 us
  Pallas kernels  34.4 us (94%)
  local copies, waits for them, and re-layouts  2.06 us (6%)
    pallas_call x1, Pallas kernels, device_fn(): pl.pallas_call(body, out_shape=jax.ShapeDtypeStruct((half, d_model), BF16...  34.4 us
    unnamed x1, local copies, waits for them, and re-layouts  2.06 us

commit v1 on v0

v1 whole, which is shorter than its diff:
```python
import jax
import jax.numpy as jnp
from jax import lax
from jax.experimental import pallas as pl
from jax.experimental.pallas import tpu as pltpu
from jax.sharding import PartitionSpec as P

MESH = pl.DeviceIdType.MESH
F32 = jnp.float32
BF16 = jnp.bfloat16
LOG2E = 1.4426950408889634

CHUNK = 128
LANES = 128
GROUPS = (1, 2, 3)


def dot(a, b):
    return jnp.dot(a, b, preferred_element_type=F32)


def split3(v):
    hi = v.astype(BF16)
    rest = v - hi.astype(F32)
    mid = rest.astype(BF16)
    return hi, mid, (rest - mid.astype(F32)).astype(BF16)


def softplus(v):
    return jnp.maximum(v, 0.0) + jnp.log1p(jnp.exp(-jnp.abs(v)))


def kernel(dims, x_hbm, wz_hbm, wx_hbm, wbc_hbm, wdt_hbm, wo_hbm, a_s, bias_s, dskip_s, out_ref,
           x_v, wz_v, wx_v, w0_v, wbc_v, wdt_v, wo_own, wo_peer, c_v, bt_v, wide_v, dt_v, ct_v, et_v, cola_v, colb_v, colc_v,
           elo_v, ehi_v, tab_v, gram_v, u_v, z_v, y_v, pf_v, pb_v, hf_v, hb_v, dec_send, dec_recv, acc_v,
           s1_send, s1_recv, s2_send, s2_recv, g_v, g_recv,
           in_sem, s1_ss, s1_rs, dec_ss, dec_rs, s2_ss, s2_rs, wy_ss, wy_rs, wf_ss, wf_rs, g_ss, g_rs):
    tokens, n_head, n_sp = dims
    d_model = x_v.shape[1]
    inner = wx_v.shape[1]
    n_chunk = tokens // CHUNK
    n_half = n_chunk // 2
    half = tokens // 2
    n_grp = len(GROUPS)
    head_dim = inner // n_head
    edge = [LANES * sum(GROUPS[:g]) for g in range(n_grp + 1)]
    wrows = inner // n_sp

    tp = lax.axis_index('tp')
    sp = lax.axis_index('sp')
    core = lax.rem(sp, 2)
    partner = sp + 1 - 2 * core
    other_tp = 1 - tp
    my_base = tp * n_half
    peer_base = other_tp * n_half

    def load(src, dst, i):
        return pltpu.make_async_copy(src, dst, in_sem.at[i])

    ld_bc = load(wbc_hbm, wbc_v, 0)
    ld_dt = load(wdt_hbm, wdt_v, 1)
    ld_x = [load(x_hbm.at[pl.ds(i * half, half)], x_v.at[pl.ds(i * half, half)], 2 + i) for i in range(2)]
    late = pl.ds(LANES, inner - LANES)
    ld_wx = load(wx_hbm.at[:, late], wx_v.at[:, late], 4)
    ld_w0 = load(wx_hbm.at[:, pl.ds(0, LANES)], w0_v.at[:, pl.ds(0, LANES)], 7)
    ld_wz = load(wz_hbm, wz_v, 5)
    ld_wo = load(wo_hbm, wo_own, 6)
    for ld in (ld_dt, ld_x[0], ld_w0, ld_x[1], ld_bc):
        ld.start()

    barrier = pltpu.get_barrier_semaphore()
    for step in range(1, n_sp):
        pl.semaphore_signal(barrier, inc=1, device_id={'sp': lax.rem(sp + step, n_sp)}, device_id_type=MESH)
    pl.semaphore_signal(barrier, inc=1, device_id={'tp': other_tp}, device_id_type=MESH)

    pl.semaphore_wait(barrier, n_sp)

    my_rows = pl.ds(sp * wrows, wrows)
    wy = pltpu.make_async_remote_copy(src_ref=wo_hbm.at[my_rows], dst_ref=wo_peer.at[my_rows], send_sem=wy_ss, recv_sem=wy_rs,
                                      device_id={'tp': other_tp}, device_id_type=MESH)
    wy.start()
    ld_wx.start()

    row_h = lax.broadcasted_iota(jnp.int32, (16, LANES), 0)
    bias_t = jnp.zeros((16, LANES), F32)
    a_t = jnp.zeros((16, LANES), F32)
    for h in range(n_head):
        bias_t = jnp.where(row_h == h, bias_s[h], bias_t)
        a_t = jnp.where(row_h == h, a_s[h] * LOG2E, a_t)
    sq_r = lax.broadcasted_iota(jnp.int32, (CHUNK, LANES), 0)
    sq_c = lax.broadcasted_iota(jnp.int32, (CHUNK, LANES), 1)
    tri = jnp.concatenate([jnp.where(sq_r <= sq_c, 1.0, 0.0), jnp.where(sq_r < sq_c, 1.0, 0.0)], axis=1).astype(BF16)
    diag2 = jnp.where(sq_r == sq_c, 2.0, 1.0)
    ex_r = lax.broadcasted_iota(jnp.int32, (LANES, inner), 0)
    ex_h = lax.broadcasted_iota(jnp.int32, (LANES, inner), 1) >> (head_dim.bit_length() - 1)
    ex_q = jnp.where((ex_r & 15) == ex_h, 1.0, 0.0)
    elo_v[...] = jnp.where(ex_r < 48, ex_q, 0.0).astype(BF16)
    ehi_v[...] = jnp.where((ex_r >= 64) & (ex_r < 112), ex_q, 0.0).astype(BF16)
    e_one = jnp.where(ex_r[:32] == ex_h[:32], 1.0, 0.0).astype(BF16)
    wide_v[...] = jnp.zeros_like(wide_v)
    ld_dt.wait()
    wide_v[0:n_head, :] = wdt_v[...].astype(F32)
    for k in range(d_model // LANES):
        rows = slice(k * LANES, (k + 1) * LANES)
        w0_v[rows, LANES:] = wide_v[:, rows].T.astype(BF16)

    ld_w0.wait()
    for i in range(2):
        ld_x[i].wait()
        rows = slice(i * half, (i + 1) * half)
        first = dot(x_v[rows, :], w0_v[...])
        u_v[rows, :LANES] = first[:, :LANES].astype(BF16)
        for k in range(n_half):
            dt_v[i * n_half + k] = softplus(first[k * CHUNK:(k + 1) * CHUNK, LANES:].T[:16] + bias_t)
    ld_bc.wait()
    for i in range(2):
        rows = slice(i * half, (i + 1) * half)
        bc_val = dot(x_v[rows, :], wbc_v[...]).astype(BF16)
        c_v[rows, :] = bc_val[:, LANES:]
        for k in range(n_half):
            bt_v[i * n_half + k] = bc_val[k * CHUNK:(k + 1) * CHUNK, :LANES].astype(F32).T.astype(BF16)

    dt_all = dt_v[...].reshape(n_chunk * 16, LANES)
    la_all = (dt_v[...] * a_t[None]).reshape(n_chunk * 16, LANES)
    cum = sum(dot(part, tri) for part in split3(la_all))
    c_log = cum[:, :LANES]
    e_log = cum[:, LANES:]
    ct_v[...] = c_log.reshape(n_chunk, 16, LANES)
    et_v[...] = e_log.reshape(n_chunk, 16, LANES)
    tail = c_log[:, LANES - 1:LANES]
    parts_ef = split3(jnp.exp2(c_log))
    parts_eb = split3(jnp.exp2(tail - e_log))
    parts_wf = split3(jnp.exp2(tail - c_log) * dt_all)
    parts_wb = split3(jnp.exp2(e_log) * dt_all)
    blank = jnp.zeros((16, LANES), F32)

    def column_tile(first, second, c):
        rows = slice(c * 16, (c + 1) * 16)
        tile = [p[rows].astype(F32) for p in first] + [blank] + [p[rows].astype(F32) for p in second] + [blank]
        return jnp.concatenate(tile, axis=0).T.astype(BF16)

    run = jnp.zeros((1, 32), F32)
    tails, starts, ends = [], [], []
    for c in range(n_chunk):
        rows = slice(c * 16, (c + 1) * 16)
        colb_v[c] = column_tile(parts_wf, parts_wb, c)
        col = jnp.concatenate([c_log[rows], e_log[rows]], axis=0).T
        colc_v[c] = col
        last = col[CHUNK - 1:CHUNK, :]
        tails.append(last)
        starts.append(run)
        run = run + last
        ends.append(run)
    logs = jnp.concatenate(tails + starts + [run - e for e in ends] + [run] * n_chunk, axis=0)
    tab = sum(dot(part, e_one) for part in split3(jnp.exp2(logs)))
    for i in range(3 * n_chunk + 1):
        tab_v[i] = tab[i:i + 1, :]
    dec_send[...] = tab[3 * n_chunk:, :]

    ld_wz.start()
    ld_wo.start()

    def to_partner(g):
        return pltpu.make_async_remote_copy(src_ref=s1_send[g], dst_ref=s1_recv[g], send_sem=s1_ss.at[g], recv_sem=s1_rs.at[g],
                                            device_id={'sp': partner}, device_id_type=MESH)

    def to_chip(g, t):
        return pltpu.make_async_remote_copy(src_ref=s2_send[g], dst_ref=s2_recv[g], send_sem=s2_ss.at[g, t], recv_sem=s2_rs.at[g],
                                            device_id={'sp': 2 - 2 * (sp // 2) + t}, device_id_type=MESH)

    def to_peer(g, k):
        return pltpu.make_async_remote_copy(src_ref=g_v[g].at[peer_base + k], dst_ref=g_recv[g].at[k], send_sem=g_ss.at[g, k],
                                            recv_sem=g_rs.at[g, k], device_id={'tp': other_tp}, device_id_type=MESH)

    def gather(step):
        return pltpu.make_async_remote_copy(src_ref=wo_peer.at[my_rows], dst_ref=wo_peer.at[my_rows], send_sem=wf_ss.at[step - 1],
                                            recv_sem=wf_rs.at[step - 1], device_id={'sp': lax.rem(sp + step, n_sp)}, device_id_type=MESH)

    dec_copy = pltpu.make_async_remote_copy(src_ref=dec_send, dst_ref=dec_recv, send_sem=dec_ss, recv_sem=dec_rs,
                                            device_id={'sp': partner}, device_id_type=MESH)
    dec_copy.start()

    def states(g):
        cols = slice(edge[g], edge[g + 1])
        if g > 0:
            for i in range(2):
                rows = slice(i * half, (i + 1) * half)
                u_v[rows, cols] = dot(x_v[rows, :], wx_v[:, cols]).astype(BF16)
        elo = elo_v[:, cols]
        ehi = ehi_v[:, cols]
        st_f, st_b = [], []
        for c in range(n_chunk):
            u_c = u_v[c * CHUNK:(c + 1) * CHUNK, cols].astype(F32)
            st_f.append(dot(bt_v[c], (u_c * dot(colb_v[c], elo)).astype(BF16)))
            st_b.append(dot(bt_v[c], (u_c * dot(colb_v[c], ehi)).astype(BF16)))
        acc = jnp.zeros((LANES, edge[g + 1] - edge[g]), F32)
        for c in range(n_chunk):
            pf_v[c, :, cols] = acc
            acc = tab_v[c][:, cols] * acc + st_f[c]
        pf_v[n_chunk, :, cols] = acc
        acc = jnp.zeros((LANES, edge[g + 1] - edge[g]), F32)
        for c in reversed(range(n_chunk)):
            pb_v[c, :, cols] = acc
            acc = tab_v[c][:, cols] * acc + st_b[c]
        pb_v[n_chunk, :, cols] = acc
        s1_send[g][...] = jnp.where(core == 0, pf_v[n_chunk, :, cols], acc).astype(BF16)
        to_partner(g).start()

    sends_far = (sp == 1) | (sp == 2)

    def pass_on(g):
        to_partner(g).wait_recv()

        @pl.when(sends_far)
        def _():
            cols = slice(edge[g], edge[g + 1])
            own = jnp.where(core == 1, pf_v[n_chunk, :, cols], pb_v[n_chunk, :, cols])
            s2_send[g][...] = (own + tab_v[3 * n_chunk][:, cols] * s1_recv[g][...].astype(F32)).astype(BF16)
            to_chip(g, 0).start()
            to_chip(g, 1).start()

    def incoming(g):
        to_chip(g, 0).wait_recv()
        cols = slice(edge[g], edge[g + 1])
        near = s1_recv[g][...].astype(F32)
        far = s2_recv[g][...].astype(F32)
        both = near + dec_recv[0:1, cols] * far
        hf_v[:, cols] = jnp.where(sp == 0, 0.0, jnp.where(sp == 1, near, jnp.where(sp == 2, far, both)))
        hb_v[:, cols] = jnp.where(sp == 3, 0.0, jnp.where(sp == 2, near, jnp.where(sp == 1, far, both)))

    lane = lax.broadcasted_iota(jnp.int32, (CHUNK, LANES), 1)
    low_lane = lane < head_dim

    def z_part(g, base):
        cols = slice(edge[g], edge[g + 1])
        rows = pl.ds(pl.multiple_of(base * CHUNK, CHUNK), half)
        z_v[rows, cols] = dot(x_v[rows, :], wz_v[:, cols]).astype(BF16)

    def intra(g, c):
        rows = pl.ds(pl.multiple_of(c * CHUNK, CHUNK), CHUNK)
        gram = gram_v[c]
        for lo in range(edge[g], edge[g + 1], LANES):
            lanes = slice(lo, lo + LANES)
            h0 = lo // head_dim
            u_pair = u_v[rows, lanes]
            weights = []
            for h in (h0, h0 + 1):
                arg = jnp.minimum(colc_v[c, :, h:h + 1] - ct_v[c, h:h + 1, :], et_v[c, h:h + 1, :] - colc_v[c, :, 16 + h:17 + h])
                weights.append((gram * jnp.exp2(arg) * dt_v[c, h:h + 1, :]).astype(BF16))
            zero = jnp.zeros_like(u_pair)
            u_diag = jnp.concatenate([jnp.where(low_lane, u_pair, zero), jnp.where(low_lane, zero, u_pair)], axis=0)
            skip = jnp.where(low_lane[:1], 2.0 * dskip_s[h0], 2.0 * dskip_s[h0 + 1])
            y_v[rows, lanes] = dot(jnp.concatenate(weights, axis=1), u_diag) + skip * u_pair.astype(F32)

    def finish(g, c):
        cols = slice(edge[g], edge[g + 1])
        rows = pl.ds(pl.multiple_of(c * CHUNK, CHUNK), CHUNK)
        in_f = (pf_v[c, :, cols] + tab_v[n_chunk + c][:, cols] * hf_v[:, cols]).astype(BF16)
        in_b = (pb_v[c, :, cols] + tab_v[2 * n_chunk + c][:, cols] * hb_v[:, cols]).astype(BF16)
        c_mat = c_v[rows, :]
        y = y_v[rows, cols] + dot(cola_v[c], elo_v[:, cols]) * dot(c_mat, in_f) + dot(cola_v[c], ehi_v[:, cols]) * dot(c_mat, in_b)
        hz = 0.5 * z_v[rows, cols].astype(F32)
        g_v[g][c] = (y * (hz + hz * jnp.tanh(hz))).astype(BF16)

    states(0)
    for c in range(n_chunk):
        gram_v[c] = dot(c_v[c * CHUNK:(c + 1) * CHUNK, :], bt_v[c]) * diag2
        cola_v[c] = column_tile(parts_ef, parts_eb, c)
    ld_wx.wait()
    states(1)
    pass_on(0)
    states(2)
    pass_on(1)
    ld_wz.wait()
    for g in range(n_grp):
        z_part(g, peer_base)
        for k in range(n_half):
            intra(g, peer_base + k)
        if g == 0:
            pass_on(2)
            dec_copy.wait_recv()
        incoming(g)
        for k in range(n_half):
            finish(g, peer_base + k)
            to_peer(g, k).start()
        if g == 0:
            wy.wait_recv()
            for step in range(1, n_sp):
                gather(step).start()

    for g in range(n_grp):
        z_part(g, my_base)
        for k in range(n_half):
            intra(g, my_base + k)
        for k in range(n_half):
            finish(g, my_base + k)
    ld_wo.wait()
    my_tokens = pl.ds(pl.multiple_of(my_base * CHUNK, CHUNK), half)
    acc_v[...] = x_v[my_tokens, :].astype(F32)
    for g in range(n_grp):
        mine = g_v[g][pl.ds(my_base, n_half)].reshape(half, edge[g + 1] - edge[g])
        acc_v[...] += dot(mine, wo_own[edge[g]:edge[g + 1], :])
    for step in range(1, n_sp):
        gather(step).wait_recv()
    for g in range(n_grp):
        w_g = wo_peer[edge[g]:edge[g + 1], :]
        for k in range(n_half):
            to_peer(g, k).wait_recv()
            rows = slice(k * CHUNK, (k + 1) * CHUNK)
            val = acc_v[rows, :] + dot(g_recv[g][k], w_g)
            if g < n_grp - 1:
                acc_v[rows, :] = val
            else:
                out_ref[rows, :] = val.astype(BF16)

    wy.wait_send()
    dec_copy.wait_send()
    for step in range(1, n_sp):
        gather(step).wait_send()
    for g in range(n_grp):
        to_partner(g).wait_send()

        @pl.when(sends_far)
        def _():
            to_chip(g, 0).wait_send()
            to_chip(g, 1).wait_send()
        for k in range(n_half):
            to_peer(g, k).wait_send()


def solution(mesh):
    n_sp = mesh.shape['sp']

    def device_fn(x_blk, w_z, w_x, w_bc, w_dt, a_neg, dt_bias, d_skip, w_out):
        tokens, d_model = x_blk.shape
        n_head = a_neg.shape[0]
        inner = w_x.shape[1]
        half = tokens // 2
        n_chunk = tokens // CHUNK
        n_half = n_chunk // 2
        n_grp = len(GROUPS)
        wide = [LANES * p for p in GROUPS]
        vmem = pltpu.VMEM
        dma = pltpu.SemaphoreType.DMA
        state = [vmem((LANES, w), BF16) for w in wide]
        hbm = pl.BlockSpec(memory_space=pltpu.HBM)
        smem = pl.BlockSpec(memory_space=pltpu.SMEM)

        def body(*refs):
            kernel((tokens, n_head, n_sp), *refs)

        return pl.pallas_call(
            body,
            out_shape=pltpu.VMEM((half, d_model), BF16),
            in_specs=[hbm] * 6 + [smem] * 3,
            out_specs=pl.BlockSpec(memory_space=pltpu.VMEM),
            scratch_shapes=[
                vmem((tokens, d_model), BF16), vmem((d_model, inner), BF16), vmem((d_model, inner), BF16), vmem((d_model, 2 * LANES), BF16),
                vmem(w_bc.shape, BF16), vmem(w_dt.shape[::-1], BF16), vmem((inner, d_model), BF16), vmem((inner, d_model), BF16),
                vmem((tokens, LANES), BF16), vmem((n_chunk, LANES, CHUNK), BF16), vmem((LANES, d_model), F32),
                vmem((n_chunk, 16, LANES), F32), vmem((n_chunk, 16, LANES), F32), vmem((n_chunk, 16, LANES), F32),
                vmem((n_chunk, CHUNK, LANES), BF16), vmem((n_chunk, CHUNK, LANES), BF16), vmem((n_chunk, CHUNK, 32), F32),
                vmem((LANES, inner), BF16), vmem((LANES, inner), BF16), vmem((3 * n_chunk + 1, 1, inner), F32),
                vmem((n_chunk, CHUNK, CHUNK), F32),
                vmem((tokens, inner), BF16), vmem((tokens, inner), BF16), vmem((tokens, inner), F32),
                vmem((n_chunk + 1, LANES, inner), F32), vmem((n_chunk + 1, LANES, inner), F32),
                vmem((LANES, inner), F32), vmem((LANES, inner), F32), vmem((8, inner), F32), vmem((8, inner), F32),
                vmem((half, d_model), F32), state, state, state, state,
                [vmem((n_chunk, CHUNK, w), BF16) for w in wide], [vmem((n_half, CHUNK, w), BF16) for w in wide],
                dma((8,)), dma((n_grp,)), dma((n_grp,)), dma, dma, dma((n_grp, 2)), dma((n_grp,)),
                dma, dma, dma((n_sp - 1,)), dma((n_sp - 1,)), dma((n_grp, n_half)), dma((n_grp, n_half)),
            ],
            compiler_params=pltpu.CompilerParams(collective_id=0, has_side_effects=True, vmem_limit_bytes=56 * 2 ** 20),
            cost_estimate=pl.CostEstimate(flops=8 * 10 ** 9, bytes_accessed=8 * 10 ** 6, transcendentals=4 * 10 ** 6),
            name='mamba_layer',
        )(x_blk, w_z, w_x, w_bc, w_dt.T, w_out, a_neg, dt_bias, d_skip)

    in_specs = (P(('dp', 'sp'), None), P(None, 'tp'), P(None, 'tp'), P(None, None), P(None, 'tp'), P('tp'), P('tp'), P('tp'), P('tp', None))
    out_specs = P(('dp', 'sp', 'tp'), None)
    return jax.shard_map(device_fn, mesh=mesh, in_specs=in_specs, out_specs=out_specs, check_vma=False)
```

time: 36.6 us -> 35.6 us (0.973)
  local copies, waits for them, and re-layouts: 2.06 us -> 0.88 us
    unnamed x1, local copies, waits for them, and re-layouts: 2.06 us -> 0.88 us
where the time goes in v1:
time: 35.6 us; the launch traced here: 35.5 us
  Pallas kernels  34.6 us (97%)
  local copies, waits for them, and re-layouts  0.88 us (2%)
    pallas_call x1, Pallas kernels, device_fn(): pl.pallas_call(body, out_shape=pltpu.VMEM((half, d_model), BF16), in_spec...  34.6 us
    unnamed x1, local copies, waits for them, and re-layouts  0.88 us

profile of v1, /device:TPU:0, one launch (start us, length us, event | category | flops | bytes accessed | tf_op | source)
XLA Modules:
  0.0 35.5 jit_solution(15659190564451121729)
XLA Ops:
  0.0 34.6 %mamba_layer.1 = bf16[512,768]{1,0:T(8,128)(2,1)S(1)} custom-call(bf16[1024,768]{1,0:T(8,128)(2,1)} %refs_0_.1, bf16[768,768]{1,0:T(8,128)(2,1)} %refs_1_.1, bf16[768,768]{1,0:T(8,128)(2,1)} %refs_2_.1, bf16[768,256]{1,0:T(8,128)(2,1)} %refs_3_.1, bf16[12,768]{1,0:T(8,128)(2,1)} %bitcast.1, bf16[768,768]{1,0:T(8,128)(2,1)} %refs_5_.1, f32[12]{0:T(128)} %refs_6_.1, ...), custom_call_target="tpu_custom_call" | custom-call | flops 8000000000 | bytes 8000000 | tf_op jit(solution)/shard_map/mamba_layer/pallas_call | solution.py:352
  34.6 0.9 %copy.11 = bf16[512,768]{1,0:T(8,128)(2,1)} copy(bf16[512,768]{1,0:T(8,128)(2,1)S(1)} %mamba_layer.1) | data formatting | bytes 1572864

commit v2 on v1

--- a/solution.py
+++ b/solution.py
@@ -31,8 +31,8 @@
 
 
 def kernel(dims, x_hbm, wz_hbm, wx_hbm, wbc_hbm, wdt_hbm, wo_hbm, a_s, bias_s, dskip_s, out_ref,
-           x_v, wz_v, wx_v, w0_v, wbc_v, wdt_v, wo_own, wo_peer, c_v, bt_v, wide_v, dt_v, ct_v, et_v, cola_v, colb_v, colc_v,
-           elo_v, ehi_v, tab_v, gram_v, u_v, z_v, y_v, pf_v, pb_v, hf_v, hb_v, dec_send, dec_recv, acc_v,
+           x_v, wz_v, wx_v, w0_v, wbc_v, wdt_v, wo_own, wo_peer, c_v, bt_v, wide_v, dt_v, ct_v, et_v, cola_v, colx_v, colb_v,
+           pick_v, tab_v, gram_v, u_v, z_v, y_v, pf_v, pb_v, hf_v, hb_v, dec_send, dec_recv, acc_v,
            s1_send, s1_recv, s2_send, s2_recv, g_v, g_recv,
            in_sem, s1_ss, s1_rs, dec_ss, dec_rs, s2_ss, s2_rs, wy_ss, wy_rs, wf_ss, wf_rs, g_ss, g_rs):
     tokens, n_head, n_sp = dims
@@ -91,12 +91,14 @@
     sq_c = lax.broadcasted_iota(jnp.int32, (CHUNK, LANES), 1)
     tri = jnp.concatenate([jnp.where(sq_r <= sq_c, 1.0, 0.0), jnp.where(sq_r < sq_c, 1.0, 0.0)], axis=1).astype(BF16)
     diag2 = jnp.where(sq_r == sq_c, 2.0, 1.0)
-    ex_r = lax.broadcasted_iota(jnp.int32, (LANES, inner), 0)
-    ex_h = lax.broadcasted_iota(jnp.int32, (LANES, inner), 1) >> (head_dim.bit_length() - 1)
-    ex_q = jnp.where((ex_r & 15) == ex_h, 1.0, 0.0)
-    elo_v[...] = jnp.where(ex_r < 48, ex_q, 0.0).astype(BF16)
-    ehi_v[...] = jnp.where((ex_r >= 64) & (ex_r < 112), ex_q, 0.0).astype(BF16)
-    e_one = jnp.where(ex_r[:32] == ex_h[:32], 1.0, 0.0).astype(BF16)
+    ex_r = lax.broadcasted_iota(jnp.int32, (LANES, 2 * inner), 0)
+    ex_c = lax.broadcasted_iota(jnp.int32, (LANES, 2 * inner), 1)
+    shift = head_dim.bit_length() - 1
+    ex_h = (((ex_c >> 8) << 7) + (ex_c & 127)) >> shift
+    ex_t = ex_r - ((ex_c & 128) >> 1)
+    pick_v[...] = jnp.where(((ex_r & 15) == ex_h) & (ex_t >= 0) & (ex_t < 48), 1.0, 0.0).astype(BF16)
+    one_r = lax.broadcasted_iota(jnp.int32, (32, inner), 0)
+    e_one = jnp.where(one_r == (lax.broadcasted_iota(jnp.int32, (32, inner), 1) >> shift), 1.0, 0.0).astype(BF16)
     wide_v[...] = jnp.zeros_like(wide_v)
     ld_dt.wait()
     wide_v[0:n_head, :] = wdt_v[...].astype(F32)
@@ -112,17 +114,19 @@
         u_v[rows, :LANES] = first[:, :LANES].astype(BF16)
         for k in range(n_half):
             dt_v[i * n_half + k] = softplus(first[k * CHUNK:(k + 1) * CHUNK, LANES:].T[:16] + bias_t)
+    dt_all = dt_v[...].reshape(n_chunk * 16, LANES)
+    la_all = (dt_v[...] * a_t[None]).reshape(n_chunk * 16, LANES)
+    cum = sum(dot(part, tri) for part in split3(la_all))
     ld_bc.wait()
-    for i in range(2):
+
+    def project_bc(i):
         rows = slice(i * half, (i + 1) * half)
         bc_val = dot(x_v[rows, :], wbc_v[...]).astype(BF16)
         c_v[rows, :] = bc_val[:, LANES:]
         for k in range(n_half):
             bt_v[i * n_half + k] = bc_val[k * CHUNK:(k + 1) * CHUNK, :LANES].astype(F32).T.astype(BF16)
 
-    dt_all = dt_v[...].reshape(n_chunk * 16, LANES)
-    la_all = (dt_v[...] * a_t[None]).reshape(n_chunk * 16, LANES)
-    cum = sum(dot(part, tri) for part in split3(la_all))
+    project_bc(0)
     c_log = cum[:, :LANES]
     e_log = cum[:, LANES:]
     ct_v[...] = c_log.reshape(n_chunk, 16, LANES)
@@ -132,20 +136,24 @@
     parts_eb = split3(jnp.exp2(tail - e_log))
     parts_wf = split3(jnp.exp2(tail - c_log) * dt_all)
     parts_wb = split3(jnp.exp2(e_log) * dt_all)
+    project_bc(1)
     blank = jnp.zeros((16, LANES), F32)
 
-    def column_tile(first, second, c):
+    def row_tile(first, second, c):
         rows = slice(c * 16, (c + 1) * 16)
         tile = [p[rows].astype(F32) for p in first] + [blank] + [p[rows].astype(F32) for p in second] + [blank]
-        return jnp.concatenate(tile, axis=0).T.astype(BF16)
+        return jnp.concatenate(tile, axis=0)
+
+    def column_tile(first, second, c):
+        return row_tile(first, second, c).T.astype(BF16)
 
     run = jnp.zeros((1, 32), F32)
     tails, starts, ends = [], [], []
     for c in range(n_chunk):
         rows = slice(c * 16, (c + 1) * 16)
         colb_v[c] = column_tile(parts_wf, parts_wb, c)
+        cola_v[c] = row_tile(parts_ef, parts_eb, c)
         col = jnp.concatenate([c_log[rows], e_log[rows]], axis=0).T
-        colc_v[c] = col
         last = col[CHUNK - 1:CHUNK, :]
         tails.append(last)
         starts.append(run)
@@ -172,38 +180,44 @@
         return pltpu.make_async_remote_copy(src_ref=g_v[g].at[peer_base + k], dst_ref=g_recv[g].at[k], send_sem=g_ss.at[g, k],
                                             recv_sem=g_rs.at[g, k], device_id={'tp': other_tp}, device_id_type=MESH)
 
-    def gather(step):
-        return pltpu.make_async_remote_copy(src_ref=wo_peer.at[my_rows], dst_ref=wo_peer.at[my_rows], send_sem=wf_ss.at[step - 1],
-                                            recv_sem=wf_rs.at[step - 1], device_id={'sp': lax.rem(sp + step, n_sp)}, device_id_type=MESH)
+    def gather(i):
+        owner = lax.rem(sp + 2, n_sp) if i == 2 else sp
+        block = wo_peer.at[pl.ds(owner * wrows, wrows)]
+        target = lax.rem(sp + 2, n_sp) if i == 1 else partner
+        return pltpu.make_async_remote_copy(src_ref=block, dst_ref=block, send_sem=wf_ss.at[i], recv_sem=wf_rs.at[i],
+                                            device_id={'sp': target}, device_id_type=MESH)
 
     dec_copy = pltpu.make_async_remote_copy(src_ref=dec_send, dst_ref=dec_recv, send_sem=dec_ss, recv_sem=dec_rs,
                                             device_id={'sp': partner}, device_id_type=MESH)
     dec_copy.start()
 
+    def project_u(g):
+        cols = slice(edge[g], edge[g + 1])
+        for i in range(2):
+            rows = slice(i * half, (i + 1) * half)
+            u_v[rows, cols] = dot(x_v[rows, :], wx_v[:, cols]).astype(BF16)
+
     def states(g):
-        cols = slice(edge[g], edge[g + 1])
-        if g > 0:
-            for i in range(2):
-                rows = slice(i * half, (i + 1) * half)
-                u_v[rows, cols] = dot(x_v[rows, :], wx_v[:, cols]).astype(BF16)
-        elo = elo_v[:, cols]
-        ehi = ehi_v[:, cols]
-        st_f, st_b = [], []
-        for c in range(n_chunk):
-            u_c = u_v[c * CHUNK:(c + 1) * CHUNK, cols].astype(F32)
-            st_f.append(dot(bt_v[c], (u_c * dot(colb_v[c], elo)).astype(BF16)))
-            st_b.append(dot(bt_v[c], (u_c * dot(colb_v[c], ehi)).astype(BF16)))
-        acc = jnp.zeros((LANES, edge[g + 1] - edge[g]), F32)
-        for c in range(n_chunk):
-            pf_v[c, :, cols] = acc
-            acc = tab_v[c][:, cols] * acc + st_f[c]
-        pf_v[n_chunk, :, cols] = acc
-        acc = jnp.zeros((LANES, edge[g + 1] - edge[g]), F32)
-        for c in reversed(range(n_chunk)):
-            pb_v[c, :, cols] = acc
-            acc = tab_v[c][:, cols] * acc + st_b[c]
-        pb_v[n_chunk, :, cols] = acc
-        s1_send[g][...] = jnp.where(core == 0, pf_v[n_chunk, :, cols], acc).astype(BF16)
+        for lo in range(edge[g], edge[g + 1], LANES):
+            cols = slice(lo, lo + LANES)
+            pick = pick_v[:, 2 * lo:2 * lo + 2 * LANES]
+            acc = jnp.zeros((LANES, LANES), F32)
+            for c in range(n_chunk):
+                u_c = u_v[c * CHUNK:(c + 1) * CHUNK, cols].astype(F32)
+                w_c = dot(colb_v[c], pick)
+                u_w = jnp.concatenate([u_c * w_c[:, :LANES], u_c * w_c[:, LANES:]], axis=1).astype(BF16)
+                st = dot(bt_v[c], u_w)
+                pf_v[c, :, cols] = acc
+                acc = tab_v[c][:, cols] * acc + st[:, :LANES]
+                pb_v[c, :, cols] = st[:, LANES:]
+            pf_v[n_chunk, :, cols] = acc
+            acc = jnp.zeros((LANES, LANES), F32)
+            for c in reversed(range(n_chunk)):
+                st = pb_v[c, :, cols]
+                pb_v[c, :, cols] = acc
+                acc = tab_v[c][:, cols] * acc + st
+            pb_v[n_chunk, :, cols] = acc
+            s1_send[g][:, lo - edge[g]:lo - edge[g] + LANES] = jnp.where(core == 0, pf_v[n_chunk, :, cols], acc).astype(BF16)
         to_partner(g).start()
 
     sends_far = (sp == 1) | (sp == 2)
@@ -230,8 +244,10 @@
 
     lane = lax.broadcasted_iota(jnp.int32, (CHUNK, LANES), 1)
     low_lane = lane < head_dim
-
-    def z_part(g, base):
+    above = sq_r < sq_c
+    below = sq_r > sq_c
+
+    def project_z(g, base):
         cols = slice(edge[g], edge[g + 1])
         rows = pl.ds(pl.multiple_of(base * CHUNK, CHUNK), half)
         z_v[rows, cols] = dot(x_v[rows, :], wz_v[:, cols]).astype(BF16)
@@ -245,51 +261,71 @@
             u_pair = u_v[rows, lanes]
             weights = []
             for h in (h0, h0 + 1):
-                arg = jnp.minimum(colc_v[c, :, h:h + 1] - ct_v[c, h:h + 1, :], et_v[c, h:h + 1, :] - colc_v[c, :, 16 + h:17 + h])
-                weights.append((gram * jnp.exp2(arg) * dt_v[c, h:h + 1, :]).astype(BF16))
+                incl = ct_v[c, h:h + 1, :]
+                excl = et_v[c, h:h + 1, :]
+                gap = jnp.where(above, incl, excl).T - jnp.where(below, incl, excl)
+                weights.append((gram * jnp.exp2(jnp.minimum(gap, -gap)) * dt_v[c, h:h + 1, :]).astype(BF16))
             zero = jnp.zeros_like(u_pair)
             u_diag = jnp.concatenate([jnp.where(low_lane, u_pair, zero), jnp.where(low_lane, zero, u_pair)], axis=0)
             skip = jnp.where(low_lane[:1], 2.0 * dskip_s[h0], 2.0 * dskip_s[h0 + 1])
             y_v[rows, lanes] = dot(jnp.concatenate(weights, axis=1), u_diag) + skip * u_pair.astype(F32)
 
     def finish(g, c):
-        cols = slice(edge[g], edge[g + 1])
         rows = pl.ds(pl.multiple_of(c * CHUNK, CHUNK), CHUNK)
-        in_f = (pf_v[c, :, cols] + tab_v[n_chunk + c][:, cols] * hf_v[:, cols]).astype(BF16)
-        in_b = (pb_v[c, :, cols] + tab_v[2 * n_chunk + c][:, cols] * hb_v[:, cols]).astype(BF16)
         c_mat = c_v[rows, :]
-        y = y_v[rows, cols] + dot(cola_v[c], elo_v[:, cols]) * dot(c_mat, in_f) + dot(cola_v[c], ehi_v[:, cols]) * dot(c_mat, in_b)
-        hz = 0.5 * z_v[rows, cols].astype(F32)
-        g_v[g][c] = (y * (hz + hz * jnp.tanh(hz))).astype(BF16)
-
-    states(0)
-    for c in range(n_chunk):
-        gram_v[c] = dot(c_v[c * CHUNK:(c + 1) * CHUNK, :], bt_v[c]) * diag2
-        cola_v[c] = column_tile(parts_ef, parts_eb, c)
-    ld_wx.wait()
-    states(1)
-    pass_on(0)
-    states(2)
-    pass_on(1)
-    ld_wz.wait()
-    for g in range(n_grp):
-        z_part(g, peer_base)
-        for k in range(n_half):
-            intra(g, peer_base + k)
-        if g == 0:
-            pass_on(2)
-            dec_copy.wait_recv()
+        for lo in range(edge[g], edge[g + 1], LANES):
+            cols = slice(lo, lo + LANES)
+            in_f = pf_v[c, :, cols] + tab_v[n_chunk + c][:, cols] * hf_v[:, cols]
+            in_b = pb_v[c, :, cols] + tab_v[2 * n_chunk + c][:, cols] * hb_v[:, cols]
+            w_c = dot(colx_v[c], pick_v[:, 2 * lo:2 * lo + 2 * LANES])
+            y_in = w_c * dot(c_mat, jnp.concatenate([in_f, in_b], axis=1).astype(BF16))
+            y = y_v[rows, cols] + y_in[:, :LANES] + y_in[:, LANES:]
+            hz = 0.5 * z_v[rows, cols].astype(F32)
+            g_v[g][c, :, lo - edge[g]:lo - edge[g] + LANES] = (y * (hz + hz * jnp.tanh(hz))).astype(BF16)
+
+    def gram_part(base):
+        for k in range(n_half):
+            c = base + k
+            colx_v[c] = cola_v[c].T.astype(BF16)
+            gram_v[c] = dot(c_v[pl.ds(pl.multiple_of(c * CHUNK, CHUNK), CHUNK), :], bt_v[c]) * diag2
+
+    def send_finished(g):
         incoming(g)
         for k in range(n_half):
             finish(g, peer_base + k)
             to_peer(g, k).start()
-        if g == 0:
-            wy.wait_recv()
-            for step in range(1, n_sp):
-                gather(step).start()
-
+
+    states(0)
+    gram_part(peer_base)
+    ld_wx.wait()
+    project_u(1)
+    pass_on(0)
+    states(1)
+    ld_wz.wait()
+    project_z(0, peer_base)
+    for k in range(n_half):
+        intra(0, peer_base + k)
+    pass_on(1)
+    project_u(2)
+    dec_copy.wait_recv()
+    send_finished(0)
+    states(2)
+    project_z(1, peer_base)
+    for k in range(n_half):
+        intra(1, peer_base + k)
+    pass_on(2)
+    send_finished(1)
+    wy.wait_recv()
+    gather(0).start()
+    gather(1).start()
+    project_z(2, peer_base)
+    for k in range(n_half):
+        intra(2, peer_base + k)
+    send_finished(2)
+
+    gram_part(my_base)
     for g in range(n_grp):
-        z_part(g, my_base)
+        project_z(g, my_base)
         for k in range(n_half):
             intra(g, my_base + k)
         for k in range(n_half):
@@ -300,8 +336,10 @@
     for g in range(n_grp):
         mine = g_v[g][pl.ds(my_base, n_half)].reshape(half, edge[g + 1] - edge[g])
         acc_v[...] += dot(mine, wo_own[edge[g]:edge[g + 1], :])
-    for step in range(1, n_sp):
-        gather(step).wait_recv()
+    gather(1).wait_recv()
+    gather(2).start()
+    gather(0).wait_recv()
+    gather(2).wait_recv()
     for g in range(n_grp):
         w_g = wo_peer[edge[g]:edge[g + 1], :]
         for k in range(n_half):
@@ -315,8 +353,8 @@
 
     wy.wait_send()
     dec_copy.wait_send()
-    for step in range(1, n_sp):
-        gather(step).wait_send()
+    for i in range(3):
+        gather(i).wait_send()
     for g in range(n_grp):
         to_partner(g).wait_send()
 
@@ -359,8 +397,8 @@
                 vmem(w_bc.shape, BF16), vmem(w_dt.shape[::-1], BF16), vmem((inner, d_model), BF16), vmem((inner, d_model), BF16),
                 vmem((tokens, LANES), BF16), vmem((n_chunk, LANES, CHUNK), BF16), vmem((LANES, d_model), F32),
                 vmem((n_chunk, 16, LANES), F32), vmem((n_chunk, 16, LANES), F32), vmem((n_chunk, 16, LANES), F32),
-                vmem((n_chunk, CHUNK, LANES), BF16), vmem((n_chunk, CHUNK, LANES), BF16), vmem((n_chunk, CHUNK, 32), F32),
-                vmem((LANES, inner), BF16), vmem((LANES, inner), BF16), vmem((3 * n_chunk + 1, 1, inner), F32),
+                vmem((n_chunk, LANES, CHUNK), F32), vmem((n_chunk, CHUNK, LANES), BF16), vmem((n_chunk, CHUNK, LANES), BF16),
+                vmem((LANES, 2 * inner), BF16), vmem((3 * n_chunk + 1, 1, inner), F32),
                 vmem((n_chunk, CHUNK, CHUNK), F32),
                 vmem((tokens, inner), BF16), vmem((tokens, inner), BF16), vmem((tokens, inner), F32),
                 vmem((n_chunk + 1, LANES, inner), F32), vmem((n_chunk + 1, LANES, inner), F32),
@@ -368,7 +406,7 @@
                 vmem((half, d_model), F32), state, state, state, state,
                 [vmem((n_chunk, CHUNK, w), BF16) for w in wide], [vmem((n_half, CHUNK, w), BF16) for w in wide],
                 dma((8,)), dma((n_grp,)), dma((n_grp,)), dma, dma, dma((n_grp, 2)), dma((n_grp,)),
-                dma, dma, dma((n_sp - 1,)), dma((n_sp - 1,)), dma((n_grp, n_half)), dma((n_grp, n_half)),
+                dma, dma, dma((3,)), dma((3,)), dma((n_grp, n_half)), dma((n_grp, n_half)),
             ],
             compiler_params=pltpu.CompilerParams(collective_id=0, has_side_effects=True, vmem_limit_bytes=56 * 2 ** 20),
             cost_estimate=pl.CostEstimate(flops=8 * 10 ** 9, bytes_accessed=8 * 10 ** 6, transcendentals=4 * 10 ** 6),

time: 35.6 us -> 32.9 us (0.924)
  Pallas kernels: 34.6 us -> 32 us
    pallas_call x1, Pallas kernels: 34.6 us -> 32 us  [device_fn(): pl.pallas_call(body, out_shape=pltpu.VMEM((half, d_model), BF16), in_spec...]
where the time goes in v2:
time: 32.9 us
  Pallas kernels  32 us (97%)
  local copies, waits for them, and re-layouts  0.88 us (3%)
    pallas_call x1, Pallas kernels, device_fn(): pl.pallas_call(body, out_shape=pltpu.VMEM((half, d_model), BF16), in_spec...  32 us
    unnamed x1, local copies, waits for them, and re-layouts  0.88 us

profile of v2, /device:TPU:0, one launch (start us, length us, event | category | flops | bytes accessed | tf_op | source)
XLA Modules:
  0.0 32.9 jit_solution(6051359232536927242)
XLA Ops:
  0.0 32.0 %mamba_layer.1 = bf16[512,768]{1,0:T(8,128)(2,1)S(1)} custom-call(bf16[1024,768]{1,0:T(8,128)(2,1)} %refs_0_.1, bf16[768,768]{1,0:T(8,128)(2,1)} %refs_1_.1, bf16[768,768]{1,0:T(8,128)(2,1)} %refs_2_.1, bf16[768,256]{1,0:T(8,128)(2,1)} %refs_3_.1, bf16[12,768]{1,0:T(8,128)(2,1)} %bitcast.1, bf16[768,768]{1,0:T(8,128)(2,1)} %refs_5_.1, f32[12]{0:T(128)} %refs_6_.1, ...), custom_call_target="tpu_custom_call" | custom-call | flops 8000000000 | bytes 8000000 | tf_op jit(solution)/shard_map/mamba_layer/pallas_call | solution.py:390
  32.0 0.9 %copy.11 = bf16[512,768]{1,0:T(8,128)(2,1)} copy(bf16[512,768]{1,0:T(8,128)(2,1)S(1)} %mamba_layer.1) | data formatting | bytes 1572864

commit v3 on v2

--- a/solution.py
+++ b/solution.py
@@ -296,19 +296,19 @@
             to_peer(g, k).start()
 
     states(0)
-    gram_part(peer_base)
     ld_wx.wait()
     project_u(1)
     pass_on(0)
+    gram_part(peer_base)
     states(1)
     ld_wz.wait()
     project_z(0, peer_base)
     for k in range(n_half):
         intra(0, peer_base + k)
     pass_on(1)
-    project_u(2)
     dec_copy.wait_recv()
     send_finished(0)
+    project_u(2)
     states(2)
     project_z(1, peer_base)
     for k in range(n_half):

time: 32.9 us -> 32.5 us (0.988)
  Pallas kernels: 32 us -> 31.5 us
    pallas_call x1, Pallas kernels: 32 us -> 31.5 us  [device_fn(): pl.pallas_call(body, out_shape=pltpu.VMEM((half, d_model), BF16), in_spec...]
where the time goes in v3:
time: 32.5 us; the launch traced here: 32.4 us
  Pallas kernels  31.5 us (97%)
  local copies, waits for them, and re-layouts  0.88 us (3%)
    pallas_call x1, Pallas kernels, device_fn(): pl.pallas_call(body, out_shape=pltpu.VMEM((half, d_model), BF16), in_spec...  31.5 us
    unnamed x1, local copies, waits for them, and re-layouts  0.88 us

profile of v3, /device:TPU:0, one launch (start us, length us, event | category | flops | bytes accessed | tf_op | source)
XLA Modules:
  0.0 32.4 jit_solution(13690292978802956039)
XLA Ops:
  0.0 31.5 %mamba_layer.1 = bf16[512,768]{1,0:T(8,128)(2,1)S(1)} custom-call(bf16[1024,768]{1,0:T(8,128)(2,1)} %refs_0_.1, bf16[768,768]{1,0:T(8,128)(2,1)} %refs_1_.1, bf16[768,768]{1,0:T(8,128)(2,1)} %refs_2_.1, bf16[768,256]{1,0:T(8,128)(2,1)} %refs_3_.1, bf16[12,768]{1,0:T(8,128)(2,1)} %bitcast.1, bf16[768,768]{1,0:T(8,128)(2,1)} %refs_5_.1, f32[12]{0:T(128)} %refs_6_.1, ...), custom_call_target="tpu_custom_call" | custom-call | flops 8000000000 | bytes 8000000 | tf_op jit(solution)/shard_map/mamba_layer/pallas_call | solution.py:390
  31.5 0.9 %copy.11 = bf16[512,768]{1,0:T(8,128)(2,1)} copy(bf16[512,768]{1,0:T(8,128)(2,1)S(1)} %mamba_layer.1) | data formatting | bytes 1572864

commit v4 on v3

--- a/solution.py
+++ b/solution.py
@@ -308,11 +308,11 @@
     pass_on(1)
     dec_copy.wait_recv()
     send_finished(0)
-    project_u(2)
-    states(2)
     project_z(1, peer_base)
     for k in range(n_half):
         intra(1, peer_base + k)
+    project_u(2)
+    states(2)
     pass_on(2)
     send_finished(1)
     wy.wait_recv()
@@ -330,14 +330,14 @@
             intra(g, my_base + k)
         for k in range(n_half):
             finish(g, my_base + k)
+    gather(1).wait_recv()
+    gather(2).start()
     ld_wo.wait()
     my_tokens = pl.ds(pl.multiple_of(my_base * CHUNK, CHUNK), half)
     acc_v[...] = x_v[my_tokens, :].astype(F32)
     for g in range(n_grp):
         mine = g_v[g][pl.ds(my_base, n_half)].reshape(half, edge[g + 1] - edge[g])
         acc_v[...] += dot(mine, wo_own[edge[g]:edge[g + 1], :])
-    gather(1).wait_recv()
-    gather(2).start()
     gather(0).wait_recv()
     gather(2).wait_recv()
     for g in range(n_grp):

time: 32.5 us -> 33 us (1.015)
  Pallas kernels: 31.5 us -> 32 us
    pallas_call x1, Pallas kernels: 31.5 us -> 32 us  [device_fn(): pl.pallas_call(body, out_shape=pltpu.VMEM((half, d_model), BF16), in_spec...]
where the time goes in v4:
time: 33 us; the launch traced here: 32.9 us
  Pallas kernels  32 us (97%)
  local copies, waits for them, and re-layouts  0.88 us (3%)
    pallas_call x1, Pallas kernels, device_fn(): pl.pallas_call(body, out_shape=pltpu.VMEM((half, d_model), BF16), in_spec...  32 us
    unnamed x1, local copies, waits for them, and re-layouts  0.88 us

profile of v4, /device:TPU:0, one launch (start us, length us, event | category | flops | bytes accessed | tf_op | source)
XLA Modules:
  0.0 32.9 jit_solution(16035422038006469203)
XLA Ops:
  0.0 32.0 %mamba_layer.1 = bf16[512,768]{1,0:T(8,128)(2,1)S(1)} custom-call(bf16[1024,768]{1,0:T(8,128)(2,1)} %refs_0_.1, bf16[768,768]{1,0:T(8,128)(2,1)} %refs_1_.1, bf16[768,768]{1,0:T(8,128)(2,1)} %refs_2_.1, bf16[768,256]{1,0:T(8,128)(2,1)} %refs_3_.1, bf16[12,768]{1,0:T(8,128)(2,1)} %bitcast.1, bf16[768,768]{1,0:T(8,128)(2,1)} %refs_5_.1, f32[12]{0:T(128)} %refs_6_.1, ...), custom_call_target="tpu_custom_call" | custom-call | flops 8000000000 | bytes 8000000 | tf_op jit(solution)/shard_map/mamba_layer/pallas_call | solution.py:390
  32.0 0.9 %copy.11 = bf16[512,768]{1,0:T(8,128)(2,1)} copy(bf16[512,768]{1,0:T(8,128)(2,1)S(1)} %mamba_layer.1) | data formatting | bytes 1572864
